TPU v7x, 32 devices: a whole 2x2x4 slice. The times are simulated.
32 devices in a mesh: groups: 2 (over y), seq: 4 (over z), tensor: 2 (over x), sub: 2 (over core).
Axes of the slice: x: 2, y: 2, z: 4, core: 2. Of those that a mesh axis runs over, the one named last changes fastest.
Arguments:
- image_tokens: bfloat16 [2048, 3072], P(('groups', 'seq')), parts along dimension 0, may hold values from -6 to 6
- text_tokens: bfloat16 [256, 3072], P(('groups', 'seq')), parts along dimension 0, may hold values from -6 to 6
- timestep: int32 [2], P('groups'), parts along dimension 0, may hold values from 0 to 49
- text_length: int32 [2], P('groups'), parts along dimension 0, may hold values from 32 to 128
- time_table: bfloat16 [50, 3072], replicated, may hold values from -6 to 6
- mod_weight: bfloat16 [3072, 18432], P('seq', ('tensor', 'sub')), may hold values from -0.109375 to 0.109375
- qkv_image: bfloat16 [3072, 6144], P('seq', ('tensor', 'sub')), as said below
- qkv_text: bfloat16 [3072, 6144], P('seq', ('tensor', 'sub')), as said below
- norm_gain: float32 [2, 2, 16, 128], P(None, None, ('tensor', 'sub')), may hold values from 1 to 6
- proj_image: bfloat16 [2048, 3072], P(('tensor', 'sub'), 'seq'), may hold values from -0.125 to 0.125
- proj_text: bfloat16 [2048, 3072], P(('tensor', 'sub'), 'seq'), may hold values from -0.125 to 0.125
Outputs:
- image_out: bfloat16 [2048, 3072], P(('groups', 'seq'), ('tensor', 'sub')), parts along dimension 0
- text_out: bfloat16 [256, 3072], P(('groups', 'seq'), ('tensor', 'sub')), parts along dimension 0
There are 2 independent parts, one for each index of `groups`. A program takes and returns all parts, laid end to end along the dimension named above; an argument that names none is the same for every part. Nothing has to cross between parts.
Inputs may be any that keep to these rules, and one draw needn't show every extreme that they name: `qkv_image`: entries of standard deviation about 1/sqrt(3072). `qkv_text`: entries of standard deviation about 1/sqrt(3072).
All inputs are finite; a program needn't handle non-finite values.
Results may differ from a plain program's by a relative error of at most 0.0085.
Values may be sent and summed in bfloat16 or wider, within the bound.
No kernel may reach another device: no remote copies, remote signals or barrier semaphores. Data moves between devices by JAX's collectives and lax.ppermute only.
A program may use at most 64 MiB of HBM per device.

v0:
```python
import jax
import jax.numpy as jnp
from jax import lax
from jax.sharding import PartitionSpec as P

EPSILON = 1e-06


def modulate(tokens, shift, scaling):
    values = tokens.astype(jnp.float32)
    center = jnp.mean(values, axis=-1, keepdims=True)
    spread = jnp.mean(jnp.square(values - center), axis=-1, keepdims=True)
    normed = (values - center) * lax.rsqrt(spread + EPSILON)
    return (normed * (1.0 + scaling) + shift).astype(jnp.bfloat16)


def head_norm(values, gain):
    return values * lax.rsqrt(jnp.mean(values * values, axis=-1, keepdims=True) + EPSILON) * gain


def split_heads(projected, gains):
    shaped = projected.reshape(projected.shape[0], -1, 3, gains.shape[-1])
    queries = head_norm(shaped[:, :, 0], gains[0]).astype(jnp.bfloat16)
    keys = head_norm(shaped[:, :, 1], gains[1]).astype(jnp.bfloat16)
    values = shaped[:, :, 2].astype(jnp.bfloat16)
    return (queries, keys, values)


def add_rows(source, shards):
    return jnp.dot(source, shards, preferred_element_type=jnp.float32)


def body(
    image_tokens,
    text_tokens,
    timestep,
    text_length,
    time_table,
    mod_weight,
    qkv_image,
    qkv_text,
    norm_gain,
    proj_image,
    proj_text,
):
    columns_all = image_tokens.shape[1]
    embedded = lax.dynamic_index_in_dim(time_table, timestep[0], 0, keepdims=False).astype(
        jnp.float32
    )
    vector = jax.nn.silu(embedded).astype(jnp.bfloat16)
    slab_rows = mod_weight.shape[0]
    vector_rows = lax.dynamic_slice_in_dim(vector, lax.axis_index("seq") * slab_rows, slab_rows)
    partial_value = jnp.dot(vector_rows[None, :], mod_weight, preferred_element_type=jnp.float32)[0]
    summed_rows = lax.psum(partial_value, "seq")
    modulation = lax.all_gather(summed_rows, ("tensor", "sub"), axis=0, tiled=True)
    modulation = modulation.reshape(2, 3, columns_all)
    hidden_image = modulate(image_tokens, modulation[0, 0], modulation[0, 1])
    hidden_text = modulate(text_tokens, modulation[1, 0], modulation[1, 1])
    image_count = image_tokens.shape[0]
    text_count = text_tokens.shape[0]
    local_rows = image_count + text_count
    projected_image = add_rows(hidden_image, lax.all_gather(qkv_image, "seq", axis=0, tiled=True))
    projected_text = add_rows(hidden_text, lax.all_gather(qkv_text, "seq", axis=0, tiled=True))
    image_q, image_k, image_v = split_heads(projected_image, norm_gain[0])
    text_q, text_k, text_v = split_heads(projected_text, norm_gain[1])
    heads_here = image_q.shape[1]
    head_size = image_q.shape[2]
    queries = jnp.concatenate([text_q, image_q], axis=0)
    keys = jnp.concatenate([text_k, image_k], axis=0)
    values = jnp.concatenate([text_v, image_v], axis=0)
    keys_values = jnp.stack([keys, values], axis=2).reshape(local_rows, heads_here * 2 * head_size)
    factor = float(head_size) ** (-0.5)
    shards = lax.all_gather(keys_values, "seq", axis=0, tiled=True)
    count = shards.shape[0]
    blocks = shards.reshape(count, heads_here, 2, head_size)
    position = jnp.arange(count, dtype=jnp.int32)
    within = position % local_rows
    owner = position // local_rows
    usable = (within >= text_count) | (owner * text_count + within < text_length[0])
    scores = (
        jnp.einsum("qhd,khd->hqk", queries, blocks[:, :, 0], preferred_element_type=jnp.float32)
        * factor
    )
    scores = jnp.where(usable[None, None, :], scores, -1e30)
    run_max = jnp.full((heads_here, local_rows), -1e30, jnp.float32)
    new_max = jnp.maximum(run_max, jnp.max(scores, axis=-1))
    probs = jnp.exp(scores - new_max[:, :, None])
    run_sum = jnp.sum(probs, axis=-1)
    totals = jnp.einsum(
        "hqk,khd->hqd",
        probs.astype(jnp.bfloat16),
        blocks[:, :, 1],
        preferred_element_type=jnp.float32,
    )
    final_max, run_sum, totals = (new_max, run_sum, totals)
    attended = (
        (totals / run_sum[:, :, None])
        .astype(jnp.bfloat16)
        .transpose(1, 0, 2)
        .reshape(local_rows, heads_here * head_size)
    )
    stacked = jnp.stack([proj_image, proj_text], axis=0)
    text_attended = attended[:text_count]
    image_attended = attended[text_count:]
    shards = lax.all_gather(stacked, "seq", axis=2, tiled=True)
    text_part = jnp.dot(text_attended, shards[1], preferred_element_type=jnp.float32)
    image_part = jnp.dot(image_attended, shards[0], preferred_element_type=jnp.float32)
    branch = jnp.concatenate([text_part, image_part], axis=0)
    summed = lax.psum_scatter(
        branch.astype(jnp.bfloat16), ("tensor", "sub"), scatter_dimension=1, tiled=True
    ).astype(jnp.float32)
    width_here = summed.shape[1]
    first = lax.axis_index(("tensor", "sub")) * width_here
    gates = lax.dynamic_slice_in_dim(modulation[:, 2], first, width_here, 1)
    image_base = lax.dynamic_slice_in_dim(image_tokens, first, width_here, 1).astype(jnp.float32)
    text_base = lax.dynamic_slice_in_dim(text_tokens, first, width_here, 1).astype(jnp.float32)
    image_out = (image_base + gates[0] * summed[text_count:]).astype(jnp.bfloat16)
    text_out = (text_base + gates[1] * summed[:text_count]).astype(jnp.bfloat16)
    return (image_out, text_out)


def solution(mesh):
    return jax.shard_map(
        body,
        mesh=mesh,
        in_specs=(
            P(("groups", "seq"), None),
            P(("groups", "seq"), None),
            P("groups"),
            P("groups"),
            P(),
            P("seq", ("tensor", "sub")),
            P("seq", ("tensor", "sub")),
            P("seq", ("tensor", "sub")),
            P(None, None, ("tensor", "sub"), None),
            P(("tensor", "sub"), "seq"),
            P(("tensor", "sub"), "seq"),
        ),
        out_specs=(
            P(("groups", "seq"), ("tensor", "sub")),
            P(("groups", "seq"), ("tensor", "sub")),
        ),
        check_vma=False,
    )
```

profile of v0, /device:TPU:0, one launch (start us, length us, event | category | flops | bytes accessed | tf_op | source)
XLA Modules:
  0.0 563.6 jit_solution(5315166292770970705)
XLA Ops:
  7.2 0.7 all-gather.8.cloned.1.call-update
  7.9 0.7 all-gather.6.cloned.1.call-update
  9.3 0.8 dynamic-slice_convert_fusion
  10.3 4.2 convolution_reduce_fusion
  14.5 27.8 %psum.7 = f32[4608]{0:T(1024)S(1)} all-reduce(f32[4608]{0:T(1024)S(1)} %convolution_reduce_fusion), channel_id=1, replica_groups=mesh['groups'=2,'seq'=4,'tensor'=2,'sub'=2] {'seq'}, use_global_device_ids=true, to_apply=%region_0.1 | all-reduce | flops 4608 | bytes 36864 | tf_op jit(solution)/shard_map/psum | solution.py:54
  42.3 5.3 all-gather
  48.5 0.6 fusion.4
  49.2 130.5 %all-gather.8.cloned.1.call-done = bf16[3072,1536]{1,0:T(8,128)(2,1)} async-done(((bf16[768,1536]{1,0:T(8,128)(2,1)}), bf16[3072,1536]{1,0:T(8,128)(2,1)}) %all-gather.8.cloned.1.call-update) | async-done | bytes 9437200 | tf_op jit(solution)/shard_map/all_gather | solution.py:62
  179.6 6.8 %fusion.11 = f32[256,1536]{0,1:T(8,128)S(1)} fusion(bf16[3072,1536]{1,0:T(8,128)(2,1)} %all-gather.8.cloned.1.call-done, bf16[256,3072]{1,0:T(8,128)(2,1)S(1)} %copy-done, f32[3072]{0:T(1024)S(1)} %bitcast.108, f32[3072]{0:T(1024)S(1)} %bitcast.109, f32[256]{0:T(256)S(1)} %add_rsqrt_fusion.4, f32[256]{0:T(256)S(1)} %broadcast_multiply_fusion), kind=kOutput, calls=%fused_computation.19 | convolution fusion | flops 2420637696 | bytes 12609536 | tf_op jit(solution)/shard_map/dot_general | solution.py:30
  186.5 1.1 copy-done.3
  187.6 158.6 %all-gather.6.cloned.1.call-done = bf16[3072,1536]{1,0:T(8,128)(2,1)} async-done(((bf16[768,1536]{1,0:T(8,128)(2,1)}), bf16[3072,1536]{1,0:T(8,128)(2,1)}) %all-gather.6.cloned.1.call-update) | async-done | bytes 9437200 | tf_op jit(solution)/shard_map/all_gather | solution.py:63
  346.2 5.5 fusion.41
  352.5 1.2 multiply_convert_fusion
  353.7 0.4 maximum_bitcast_fusion
  354.3 0.7 copy.58
  355.0 1.3 reshape.144
  356.3 2.6 pad_maximum_fusion.1
  359.9 1.1 slice.128
  361.8 42.8 %all-gather.10.cloned.1.call-done = bf16[1152,1024]{1,0:T(8,128)(2,1)} async-done(((bf16[288,1024]{1,0:T(8,128)(2,1)}), bf16[1152,1024]{1,0:T(8,128)(2,1)}) %all-gather.10.cloned.1.call-update) | async-done | bytes 2359312 | tf_op jit(solution)/shard_map/all_gather | solution.py:73
  404.6 4.3 copy.59
  408.9 2.3 fusion.63
  411.2 1.1 fusion
  412.3 0.8 copy-done.1
  413.1 1.0 fusion.23
  414.3 105.8 %all-gather.12.cloned.1.call-done = bf16[2,512,3072]{2,1,0:T(8,128)(2,1)} async-done(((bf16[2,512,768]{2,1,0:T(8,128)(2,1)}), bf16[2,512,3072]{2,1,0:T(8,128)(2,1)}) %all-gather.12.cloned.1.call-update) | async-done | bytes 6291472 | tf_op jit(solution)/shard_map/all_gather | solution.py:105
  520.1 2.5 convolution_convert_fusion.1
  522.7 2.9 convolution_convert_fusion
  525.6 1.3 pad_maximum_fusion
  527.0 27.5 %reduce-scatter.2.cloned.1.call-done = bf16[288,768]{1,0:T(8,128)(2,1)} async-done(((bf16[288,3072]{1,0:T(8,128)(2,1)}), bf16[288,768]{1,0:T(8,128)(2,1)}) %reduce-scatter.2.cloned.1.call-update) | async-done | bytes 442384 | tf_op jit(solution)/shard_map/reduce_scatter | solution.py:109
  554.5 1.1 convert_element_type.80
  555.6 0.9 fusion.27
  556.4 0.6 fusion.48
  (55 shorter events, 3.6 us)
Async XLA Ops:
  7.2 172.5 %all-gather.8.cloned.1.call-start = ((), (), s32[]{:S(2)}) async-start(), calls=%async_computation.2 | async-start | bytes 11796480 | tf_op jit(solution)/shard_map/all_gather | solution.py:62
  7.9 338.3 %all-gather.6.cloned.1.call-start = ((), (), s32[]{:S(2)}) async-start(), calls=%async_computation.1 | async-start | bytes 11796480 | tf_op jit(solution)/shard_map/all_gather | solution.py:63
  8.6 395.9 %all-gather.10.cloned.1.call-start = ((), (), s32[]{:S(2)}) async-start(), calls=%async_computation.3 | async-start | bytes 2949120 | tf_op jit(solution)/shard_map/all_gather | solution.py:73
  10.3 37.6 %copy-start.2 = (bf16[32,3072]{1,0:T(8,128)(2,1)S(1)}, bf16[32,3072]{1,0:T(8,128)(2,1)}, u32[]{:S(2)}) copy-start(bf16[32,3072]{1,0:T(8,128)(2,1)} %param.12) | copy-start | bytes 589828
  10.3 37.9 %copy-start = (bf16[256,3072]{1,0:T(8,128)(2,1)S(1)}, bf16[256,3072]{1,0:T(8,128)(2,1)}, u32[]{:S(2)}) copy-start(bf16[256,3072]{1,0:T(8,128)(2,1)} %param.11) | copy-start | bytes 4718596
  14.5 34.6 %copy-start.4 = (f32[2,2,4,128]{3,2,1,0:T(4,128)S(1)}, f32[2,2,4,128]{3,2,1,0:T(4,128)}, u32[]{:S(2)}) copy-start(f32[2,2,4,128]{3,2,1,0:T(4,128)} %param.19) | copy-start | bytes 24580
  186.4 1.2 copy-start.3
  356.3 163.9 %all-gather.12.cloned.1.call-start = ((), (), s32[]{:S(2)}) async-start(), calls=%async_computation.4 | async-start | bytes 7864320 | tf_op jit(solution)/shard_map/all_gather | solution.py:105
  359.0 195.5 %reduce-scatter.2.cloned.1.call-start = ((), (), s32[]{:S(2)}) async-start(), calls=%async_computation.5 | async-start | bytes 2211840 | tf_op jit(solution)/shard_map/reduce_scatter | solution.py:109
  411.2 1.9 copy-start.1
Sparse Core Ops, SparseCore 0:
  9.5 170.0 all-gather.7
  181.2 164.9 all-gather.5
  356.4 48.1 all-gather.9
  406.0 114.0 all-gather.11
  527.0 27.4 reduce-scatter.1
where the time goes:
time: 564 us
  waiting for transfers between devices  467 us (83%)
  blocking collectives  33.1 us (6%)
  matrix products  25.1 us (4%)
  between operations  15.4 us (3%)
  other arithmetic  12.6 us (2%)
  local copies, waits for them, and re-layouts  10.4 us (2%)
    all_gather x1, waiting for transfers between devices, body(): lax.all_gather(qkv_text, 'seq', axis=0, tiled=True)  159 us
    all_gather x1, waiting for transfers between devices, body(): lax.all_gather(qkv_image, 'seq', axis=0, tiled=True)  130 us
    all_gather x1, waiting for transfers between devices, body(): shards = lax.all_gather(stacked, 'seq', axis=2, tiled=True)  106 us
    all_gather x1, waiting for transfers between devices, body(): shards = lax.all_gather(keys_values, 'seq', axis=0, tiled=True)  42.8 us
    psum x1, blocking collectives, body(): summed_rows = lax.psum(partial_value, 'seq')  27.8 us
    reduce_scatter x1, waiting for transfers between devices, body(): lax.psum_scatter(branch.astype(jnp.bfloat16), ('tensor', 'sub'), scatter_...  27.5 us
    dot_general x2, matrix products, add_rows(): return jnp.dot(source, shards, preferred_element_type=jnp.float32)  12.2 us
  transfers between devices with their start and end apart: 5, of which 5 were waited for; matrix products, arithmetic and copies ran while one was open for 5% of the time, Pallas kernels for 0%

commit v1 on v0

--- a/solution.py
+++ b/solution.py
@@ -4,6 +4,16 @@
 from jax.sharding import PartitionSpec as P
 
 EPSILON = 1e-06
+
+
+def gather_by_hops(x, mesh_axis, dim):
+    n_dev = lax.axis_size(mesh_axis)
+    moving, tiles = (x, [x])
+    for _ in range(n_dev - 1):
+        moving = lax.ppermute(moving, mesh_axis, [(i, (i + 1) % n_dev) for i in range(n_dev)])
+        tiles.insert(0, moving)
+    line = jnp.concatenate(tiles, axis=dim)
+    return jnp.roll(line, (lax.axis_index(mesh_axis) + 1) * x.shape[dim], axis=dim)
 
 
 def modulate(tokens, shift, scaling):
@@ -70,7 +80,7 @@
     values = jnp.concatenate([text_v, image_v], axis=0)
     keys_values = jnp.stack([keys, values], axis=2).reshape(local_rows, heads_here * 2 * head_size)
     factor = float(head_size) ** (-0.5)
-    shards = lax.all_gather(keys_values, "seq", axis=0, tiled=True)
+    shards = gather_by_hops(keys_values, "seq", 0)
     count = shards.shape[0]
     blocks = shards.reshape(count, heads_here, 2, head_size)
     position = jnp.arange(count, dtype=jnp.int32)

time: 564 us -> 544 us (0.965)
  waiting for transfers between devices: 467 us -> 427 us
  starting transfers between devices: 0.38 us -> 25 us
    ppermute x0 -> x3, waiting for transfers between devices: none -> 80.1 us  [gather_by_hops(): lax.ppermute(moving, mesh_axis, [(i, (i + 1) % n_dev) for i in range(n_de...]
    all_gather x1, waiting for transfers between devices: 106 us -> 27.2 us  [body(): shards = lax.all_gather(stacked, 'seq', axis=2, tiled=True)]
    all_gather x1 -> x0, waiting for transfers between devices: 42.8 us -> none  [body(): shards = lax.all_gather(keys_values, 'seq', axis=0, tiled=True)]
    all_gather x1, waiting for transfers between devices: 130 us -> 160 us  [body(): lax.all_gather(qkv_image, 'seq', axis=0, tiled=True)]
    all_gather x1, waiting for transfers between devices: 159 us -> 130 us  [body(): lax.all_gather(qkv_text, 'seq', axis=0, tiled=True)]
    ppermute x0 -> x3, starting transfers between devices: none -> 24.8 us  [gather_by_hops(): lax.ppermute(moving, mesh_axis, [(i, (i + 1) % n_dev) for i in range(n_de...]
  transfers between devices with their start and end apart: 5 -> 7, of which waited for: 5 -> 7; matrix products, arithmetic and copies ran while one was open for 5% -> 6% of each run, Pallas kernels for 0% -> 0%
where the time goes in v1:
time: 544 us
  waiting for transfers between devices  427 us (78%)
  blocking collectives  32 us (6%)
  matrix products  25.1 us (5%)
  starting transfers between devices  25 us (5%)
  between operations  15.5 us (3%)
  other arithmetic  11.3 us (2%)
  local copies, waits for them, and re-layouts  7.94 us (1%)
    all_gather x1, waiting for transfers between devices, body(): lax.all_gather(qkv_image, 'seq', axis=0, tiled=True)  160 us
    all_gather x1, waiting for transfers between devices, body(): lax.all_gather(qkv_text, 'seq', axis=0, tiled=True)  130 us
    ppermute x3, waiting for transfers between devices, gather_by_hops(): lax.ppermute(moving, mesh_axis, [(i, (i + 1) % n_dev) for i in range(n_de...  80.1 us
    reduce_scatter x1, waiting for transfers between devices, body(): lax.psum_scatter(branch.astype(jnp.bfloat16), ('tensor', 'sub'), scatter_...  27.5 us
    all_gather x1, waiting for transfers between devices, body(): shards = lax.all_gather(stacked, 'seq', axis=2, tiled=True)  27.2 us
    psum x1, blocking collectives, body(): summed_rows = lax.psum(partial_value, 'seq')  26.7 us
    ppermute x3, starting transfers between devices, gather_by_hops(): lax.ppermute(moving, mesh_axis, [(i, (i + 1) % n_dev) for i in range(n_de...  24.8 us
    dot_general x2, matrix products, add_rows(): return jnp.dot(source, shards, preferred_element_type=jnp.float32)  12.2 us
  transfers between devices with their start and end apart: 7, of which 7 were waited for; matrix products, arithmetic and copies ran while one was open for 6% of the time, Pallas kernels for 0%

profile of v1, /device:TPU:0, one launch (start us, length us, event | category | flops | bytes accessed | tf_op | source)
XLA Modules:
  0.0 543.7 jit_solution(3345285950190533545)
XLA Ops:
  7.2 0.7 all-gather.5.cloned.1.call-update
  8.0 0.7 all-gather.7.cloned.1.call-update
  8.7 1.4 pad_maximum_fusion.1
  10.8 0.8 dynamic-slice_convert_fusion
  11.8 4.2 convolution_reduce_fusion
  16.0 26.7 %psum.7 = f32[4608]{0:T(1024)S(1)} all-reduce(f32[4608]{0:T(1024)S(1)} %convolution_reduce_fusion), channel_id=1, replica_groups=mesh['groups'=2,'seq'=4,'tensor'=2,'sub'=2] {'seq'}, use_global_device_ids=true, to_apply=%region_0.1 | all-reduce | flops 4608 | bytes 36864 | tf_op jit(solution)/shard_map/psum | solution.py:64
  43.4 5.3 all-gather
  49.6 130.2 %all-gather.5.cloned.1.call-done = bf16[3072,1536]{1,0:T(8,128)(2,1)} async-done(((bf16[768,1536]{1,0:T(8,128)(2,1)}), bf16[3072,1536]{1,0:T(8,128)(2,1)}) %all-gather.5.cloned.1.call-update) | async-done | bytes 9437200 | tf_op jit(solution)/shard_map/all_gather | solution.py:73
  179.7 5.5 %fusion.41 = f32[32,1536]{1,0:T(8,128)S(1)} fusion(bf16[3072,1536]{1,0:T(8,128)(2,1)} %all-gather.5.cloned.1.call-done, bf16[32,3072]{1,0:T(8,128)(2,1)S(1)} %copy-done.2, f32[3072]{0:T(1024)S(1)} %bitcast.106, f32[3072]{0:T(1024)S(1)} %bitcast.105, f32[32]{0:T(128)S(1)} %add_rsqrt_fusion.5, f32[32]{0:T(128)S(1)} %broadcast_multiply_fusion.1), kind=kOutput, calls=%fused_computation.58 | convolution fusion | flops 302579712 | bytes 9855232 | tf_op jit(solution)/shard_map/dot_general | solution.py:40
  186.0 160.4 %all-gather.7.cloned.1.call-done = bf16[3072,1536]{1,0:T(8,128)(2,1)} async-done(((bf16[768,1536]{1,0:T(8,128)(2,1)}), bf16[3072,1536]{1,0:T(8,128)(2,1)}) %all-gather.7.cloned.1.call-update) | async-done | bytes 9437200 | tf_op jit(solution)/shard_map/all_gather | solution.py:72
  346.5 6.8 %fusion.11 = f32[256,1536]{0,1:T(8,128)S(1)} fusion(bf16[3072,1536]{1,0:T(8,128)(2,1)} %all-gather.7.cloned.1.call-done, bf16[256,3072]{1,0:T(8,128)(2,1)S(1)} %copy-done, f32[3072]{0:T(1024)S(1)} %bitcast.108, f32[3072]{0:T(1024)S(1)} %bitcast.109, f32[256]{0:T(256)S(1)} %add_rsqrt_fusion.4, f32[256]{0:T(256)S(1)} %broadcast_multiply_fusion), kind=kOutput, calls=%fused_computation.19 | convolution fusion | flops 2420637696 | bytes 12609536 | tf_op jit(solution)/shard_map/dot_general | solution.py:40
  354.5 0.7 copy.58
  355.7 30.3 %collective-permute-done = bf16[288,1024]{1,0:T(8,128)(2,1)S(1)} collective-permute-done((bf16[288,1024]{1,0:T(8,128)(2,1)S(1)}, bf16[288,1024]{1,0:T(8,128)(2,1)S(1)}, u32[]{:S(2)}, u32[]{:S(2)}) %collective-permute-start) | collective-permute-done | bytes 589856 | tf_op jit(solution)/shard_map/ppermute | solution.py:13
  386.0 8.5 %collective-permute-start.1 = (bf16[288,1024]{1,0:T(8,128)(2,1)S(1)}, bf16[288,1024]{1,0:T(8,128)(2,1)S(1)}, u32[]{:S(2)}, u32[]{:S(2)}) collective-permute-start(bf16[288,1024]{1,0:T(8,128)(2,1)S(1)} %collective-permute-done), channel_id=1, source_target_pairs={{0,4},{4,8},{8,12},{12,0},{1,5},{5,9},{9,13},{13,1},{2,6},{6,10},{... | collective-permute-start | bytes 1769480 | tf_op jit(solution)/shard_map/ppermute | solution.py:13
  395.2 1.1 slice.128
  396.8 23.2 %collective-permute-done.1 = bf16[288,1024]{1,0:T(8,128)(2,1)S(1)} collective-permute-done((bf16[288,1024]{1,0:T(8,128)(2,1)S(1)}, bf16[288,1024]{1,0:T(8,128)(2,1)S(1)}, u32[]{:S(2)}, u32[]{:S(2)}) %collective-permute-start.1) | collective-permute-done | bytes 589856 | tf_op jit(solution)/shard_map/ppermute | solution.py:13
  420.0 16.3 %collective-permute-start.2 = (bf16[288,1024]{1,0:T(8,128)(2,1)S(1)}, bf16[288,1024]{1,0:T(8,128)(2,1)S(1)}, u32[]{:S(2)}, u32[]{:S(2)}) collective-permute-start(bf16[288,1024]{1,0:T(8,128)(2,1)S(1)} %collective-permute-done.1), channel_id=1, source_target_pairs={{0,4},{4,8},{8,12},{12,0},{1,5},{5,9},{9,13},{13,1},{2,6},{6,10},{... | collective-permute-start | bytes 1769480 | tf_op jit(solution)/shard_map/ppermute | solution.py:13
  436.6 26.7 %collective-permute-done.2 = bf16[288,1024]{1,0:T(8,128)(2,1)S(1)} collective-permute-done((bf16[288,1024]{1,0:T(8,128)(2,1)S(1)}, bf16[288,1024]{1,0:T(8,128)(2,1)S(1)}, u32[]{:S(2)}, u32[]{:S(2)}) %collective-permute-start.2) | collective-permute-done | bytes 589856 | tf_op jit(solution)/shard_map/ppermute | solution.py:13
  463.6 0.7 constant_dynamic-slice_fusion
  464.3 2.6 copy.59
  466.8 2.3 fusion.63
  469.2 1.1 fusion
  470.3 0.6 copy-done.1
  470.8 1.0 fusion.23
  472.0 27.2 %all-gather.9.cloned.1.call-done = bf16[2,512,3072]{2,1,0:T(8,128)(2,1)} async-done(((bf16[2,512,768]{2,1,0:T(8,128)(2,1)}), bf16[2,512,3072]{2,1,0:T(8,128)(2,1)}) %all-gather.9.cloned.1.call-update) | async-done | bytes 6291472 | tf_op jit(solution)/shard_map/all_gather | solution.py:115
  499.2 2.5 convolution_convert_fusion.1
  501.8 2.9 convolution_convert_fusion
  504.7 1.3 pad_maximum_fusion
  506.1 27.5 %reduce-scatter.2.cloned.1.call-done = bf16[288,768]{1,0:T(8,128)(2,1)} async-done(((bf16[288,3072]{1,0:T(8,128)(2,1)}), bf16[288,768]{1,0:T(8,128)(2,1)}) %reduce-scatter.2.cloned.1.call-update) | async-done | bytes 442384 | tf_op jit(solution)/shard_map/reduce_scatter | solution.py:119
  533.6 1.1 convert_element_type.80
  534.7 0.6 fusion.48
  535.3 1.8 fusion.27
  (71 shorter events, 5.8 us)
Async XLA Ops:
  7.2 1.6 copy-start.5
  7.2 1.6 copy-start.4
  7.2 172.5 %all-gather.5.cloned.1.call-start = ((), (), s32[]{:S(2)}) async-start(), calls=%async_computation.1 | async-start | bytes 11796480 | tf_op jit(solution)/shard_map/all_gather | solution.py:73
  7.9 338.5 %all-gather.7.cloned.1.call-start = ((), (), s32[]{:S(2)}) async-start(), calls=%async_computation.2 | async-start | bytes 11796480 | tf_op jit(solution)/shard_map/all_gather | solution.py:72
  8.7 490.6 %all-gather.9.cloned.1.call-start = ((), (), s32[]{:S(2)}) async-start(), calls=%async_computation.3 | async-start | bytes 7864320 | tf_op jit(solution)/shard_map/all_gather | solution.py:115
  10.1 523.5 %reduce-scatter.2.cloned.1.call-start = ((), (), s32[]{:S(2)}) async-start(), calls=%async_computation.4 | async-start | bytes 2211840 | tf_op jit(solution)/shard_map/reduce_scatter | solution.py:119
  11.8 31.0 %copy-start.2 = (bf16[32,3072]{1,0:T(8,128)(2,1)S(1)}, bf16[32,3072]{1,0:T(8,128)(2,1)}, u32[]{:S(2)}) copy-start(bf16[32,3072]{1,0:T(8,128)(2,1)} %param.12) | copy-start | bytes 589828
  11.8 31.3 %copy-start = (bf16[256,3072]{1,0:T(8,128)(2,1)S(1)}, bf16[256,3072]{1,0:T(8,128)(2,1)}, u32[]{:S(2)}) copy-start(bf16[256,3072]{1,0:T(8,128)(2,1)} %param.11) | copy-start | bytes 4718596
  15.9 33.5 %copy-start.6 = (f32[2,2,4,128]{3,2,1,0:T(4,128)S(1)}, f32[2,2,4,128]{3,2,1,0:T(4,128)}, u32[]{:S(2)}) copy-start(f32[2,2,4,128]{3,2,1,0:T(4,128)} %param.19) | copy-start | bytes 24580
  353.2 1.2 copy-start.3
  355.7 30.4 %collective-permute-start = (bf16[288,1024]{1,0:T(8,128)(2,1)S(1)}, bf16[288,1024]{1,0:T(8,128)(2,1)S(1)}, u32[]{:S(2)}, u32[]{:S(2)}) collective-permute-start(bf16[288,1024]{1,0:T(8,128)(2,1)S(1)} %reshape.144), channel_id=1, source_target_pairs={{0,4},{4,8},{8,12},{12,0},{1,5},{5,9},{9,13},{13,1},{2,6},{6,10},{... | collective-permute-start | bytes 1769480 | tf_op jit(solution)/shard_map/ppermute | solution.py:13
  386.0 33.9 %collective-permute-start.1 = (bf16[288,1024]{1,0:T(8,128)(2,1)S(1)}, bf16[288,1024]{1,0:T(8,128)(2,1)S(1)}, u32[]{:S(2)}, u32[]{:S(2)}) collective-permute-start(bf16[288,1024]{1,0:T(8,128)(2,1)S(1)} %collective-permute-done), channel_id=1, source_target_pairs={{0,4},{4,8},{8,12},{12,0},{1,5},{5,9},{9,13},{13,1},{2,6},{6,10},{... | collective-permute-start | bytes 1769480 | tf_op jit(solution)/shard_map/ppermute | solution.py:13
  420.0 43.3 %collective-permute-start.2 = (bf16[288,1024]{1,0:T(8,128)(2,1)S(1)}, bf16[288,1024]{1,0:T(8,128)(2,1)S(1)}, u32[]{:S(2)}, u32[]{:S(2)}) collective-permute-start(bf16[288,1024]{1,0:T(8,128)(2,1)S(1)} %collective-permute-done.1), channel_id=1, source_target_pairs={{0,4},{4,8},{8,12},{12,0},{1,5},{5,9},{9,13},{13,1},{2,6},{6,10},{... | collective-permute-start | bytes 1769480 | tf_op jit(solution)/shard_map/ppermute | solution.py:13
  469.2 1.7 copy-start.1
Sparse Core Ops, SparseCore 0:
  9.6 170.1 all-gather.4
  181.3 165.1 all-gather.6
  348.0 151.1 all-gather.8
  506.1 27.4 reduce-scatter.1
